TPU v7x, 32 devices: a 4x4x1 block of a 4x4x8 slice. The times are simulated.
32 devices in a mesh: rep: 1 (over z), ep: 4 (over y), fsdp: 8 (over x, core).
Axes of the slice: x: 4, y: 4, z: 1, core: 2. Of those that a mesh axis runs over, the one named last changes fastest.
The devices are a block of a 4x4x8 slice.
Arguments:
- x_in: bfloat16 [16384, 2048], P(('rep', 'ep', 'fsdp'))
- norm_w: float32 [2, 2048], replicated
- router_w: bfloat16 [2, 2048, 4], replicated
- gate_w: bfloat16 [2, 4, 2048, 5632], P(None, 'ep', None, 'fsdp')
- up_w: bfloat16 [2, 4, 2048, 5632], P(None, 'ep', None, 'fsdp')
- down_w: bfloat16 [2, 4, 5632, 2048], P(None, 'ep', 'fsdp')
- routes: int32 [2, 16384, 2], P(None, ('rep', 'ep', 'fsdp'))
Outputs:
- output: bfloat16 [16384, 2048], P(('rep', 'ep', 'fsdp'))
All inputs are finite; a program needn't handle non-finite values.
Results may differ from a plain program's by a relative error of at most 0.012462.
Values are sent between devices in bfloat16 or wider.
A program may use at most 768 MiB of HBM per device.

v0:
```python
import jax
import jax.numpy as jnp
from jax import lax
from jax.sharding import PartitionSpec as P

NORM_EPS = 1e-5


def rms_norm(stream, norm_row):
    widened = stream.astype(jnp.float32)
    inv_rms = lax.rsqrt(jnp.mean(widened * widened, axis=-1, keepdims=True) + NORM_EPS)
    return (widened * inv_rms * norm_row).astype(jnp.bfloat16)


def route_gates(hidden, router_l, routes_l):
    logits = jnp.dot(hidden, router_l, preferred_element_type=jnp.float32)
    return jax.nn.softmax(jnp.take_along_axis(logits, routes_l, axis=-1), axis=-1)


def capacity_of(tok_dev, top_k, experts):
    return 8 * ((2 * tok_dev * top_k + 8 * experts - 1) // (8 * experts))


def slot_plan(routes_l, experts, capacity, owners):
    tok_dev, top_k = routes_l.shape
    flat_ids = routes_l.reshape(-1)
    onehot = (flat_ids[:, None] == jnp.arange(experts, dtype=flat_ids.dtype)[None, :]).astype(jnp.int32)
    pair_rank = jnp.sum((jnp.cumsum(onehot, axis=0) - 1) * onehot, axis=1)
    n_local = experts // owners
    pair_slot = ((flat_ids % n_local) * owners + flat_ids // n_local) * capacity + pair_rank
    pair_token = jnp.arange(tok_dev * top_k, dtype=jnp.int32) // top_k
    slot_token = jnp.zeros((experts * capacity,), jnp.int32).at[pair_slot].set(pair_token)
    return pair_slot, slot_token


def expert_ffn(expert_rows, gate_full, up_full, down_full):
    pre_gate = jnp.einsum("erd,edf->erf", expert_rows, gate_full, preferred_element_type=jnp.float32)
    pre_up = jnp.einsum("erd,edf->erf", expert_rows, up_full, preferred_element_type=jnp.float32)
    inner_act = (jax.nn.silu(pre_gate) * pre_up).astype(jnp.bfloat16)
    return jnp.einsum("erf,efd->erd", inner_act, down_full, preferred_element_type=jnp.float32).astype(jnp.bfloat16)


def combine(stream, gate_probs, pair_out):
    mixed_sum = jnp.sum(gate_probs[..., None] * pair_out.astype(jnp.float32), axis=-2)
    return (stream.astype(jnp.float32) + mixed_sum).astype(jnp.bfloat16)


def solution(mesh):
    owners = mesh.shape["ep"]
    token_spec = P(("rep", "ep", "fsdp"), None)
    expert_in_spec = P(None, "ep", None, "fsdp")
    expert_out_spec = P(None, "ep", "fsdp", None)
    route_spec = P(None, ("rep", "ep", "fsdp"), None)

    def device_step(x_in, norm_w, router_w, gate_w, up_w, down_w, routes):
        layers, tok_dev, top_k = routes.shape
        experts = router_w.shape[2]
        n_local = gate_w.shape[1]
        d_model = x_in.shape[1]
        capacity = capacity_of(tok_dev, top_k, experts)
        stream = x_in
        for layer_idx in range(layers):
            routes_l = routes[layer_idx]
            hidden = rms_norm(stream, norm_w[layer_idx])
            gate_probs = route_gates(hidden, router_w[layer_idx], routes_l)
            pair_slot, slot_token = slot_plan(routes_l, experts, capacity, owners)
            send_buf = hidden[slot_token].reshape(n_local, owners, capacity, d_model)
            recv_buf = lax.all_to_all(send_buf, "ep", 1, 1, tiled=True)
            gate_full = lax.all_gather(gate_w[layer_idx], "fsdp", axis=2, tiled=True)
            up_full = lax.all_gather(up_w[layer_idx], "fsdp", axis=2, tiled=True)
            down_full = lax.all_gather(down_w[layer_idx], "fsdp", axis=1, tiled=True)
            expert_out = expert_ffn(recv_buf.reshape(n_local, owners * capacity, d_model), gate_full, up_full, down_full)
            back_buf = lax.all_to_all(expert_out.reshape(n_local, owners, capacity, d_model), "ep", 1, 1, tiled=True)
            pair_out = back_buf.reshape(experts * capacity, d_model)[pair_slot].reshape(tok_dev, top_k, d_model)
            stream = combine(stream, gate_probs, pair_out)
        return stream

    return jax.shard_map(device_step, mesh=mesh,
                         in_specs=(token_spec, P(), P(), expert_in_spec, expert_in_spec, expert_out_spec, route_spec),
                         out_specs=token_spec, check_vma=False)
```

profile of v0, /device:TPU:98, one launch (start us, length us, event | category | flops | bytes accessed | tf_op | source)
XLA Modules:
  0.0 984.5 jit_solution(4879802072323744921)
XLA Ops:
  6.6 6.2 fusion.54
  12.9 6.2 fusion.53
  19.3 6.3 fusion.52
  25.7 0.6 all-gather.19.cloned.1.call-update
  26.3 0.6 all-gather.21.cloned.1.call-update
  26.9 0.6 fusion.56
  28.0 1.1 reduce-window.14
  29.9 4.3 scatter_custom_fusion
  34.2 0.5 fusion.16
  34.8 0.6 fusion.55
  35.4 2.1 fusion.18
  37.5 11.0 %gather_fusion = bf16[2048,2048]{1,0:T(8,128)(2,1)} fusion(bf16[512,2048]{1,0:T(8,128)(2,1)S(1)} %fusion.18, s32[2048]{0:T(1024)S(1)} %fusion.40), kind=kCustom, calls=%fused_computation.2 | custom fusion | bytes 16785408 | tf_op jit(solution)/shard_map/gather | solution.py:67
  48.5 5.9 all-to-all-start
  54.5 0.6 all-gather.23.cloned.1.call-update
  55.1 94.4 %all-to-all-done = bf16[1,4,512,2048]{3,2,0,1:T(8,128)(2,1)} async-done(((bf16[1,4,512,2048]{3,2,0,1:T(8,128)(2,1)}), bf16[1,4,512,2048]{3,2,0,1:T(8,128)(2,1)}, u32[]{:S(2)}, u32[]{:S(2)}) %all-to-all-start) | async-done | bytes 8388640 | tf_op jit(solution)/shard_map/all_to_all | solution.py:68
  149.4 56.5 %fusion.8 = f32[2048,5632]{1,0:T(8,128)} fusion(bf16[2048,2048]{1,0:T(8,128)(2,1)} %bitcast.9, bf16[1,1,2048,5632]{2,3,1,0:T(8,128)(2,1)} %all-gather.13.cloned.1.call-done), kind=kOutput, calls=%fused_computation.18 | convolution fusion | flops 47244640256 | bytes 77594624 | tf_op jit(solution)/shard_map/erd,edf->erf/dot_general | solution.py:37
  205.9 31.1 %all-gather.15.cloned.1.call-done = bf16[1,1,2048,5632]{2,3,1,0:T(8,128)(2,1)} async-done(((bf16[1,1,2048,704]{2,3,1,0:T(8,128)(2,1)}), bf16[1,1,2048,5632]{2,3,1,0:T(8,128)(2,1)}) %all-gather.15.cloned.1.call-update) | async-done | bytes 23068688 | tf_op jit(solution)/shard_map/all_gather | solution.py:70
  237.0 68.8 %multiply_convert_fusion.1 = bf16[2048,5632]{1,0:T(8,128)(2,1)} fusion(f32[2048,5632]{1,0:T(8,128)} %fusion.8, bf16[2048,2048]{1,0:T(8,128)(2,1)} %bitcast.9, bf16[1,1,2048,5632]{2,3,1,0:T(8,128)(2,1)} %all-gather.15.cloned.1.call-done), kind=kOutput, calls=%fused_computation.9 | convolution fusion | flops 47313846272 | bytes 100663296 | tf_op jit(solution)/shard_map/erd,edf->erf/dot_general | solution.py:38
  305.8 43.0 %all-gather.17.cloned.1.call-done = bf16[1,1,5632,2048]{3,2,1,0:T(8,128)(2,1)} async-done(((bf16[1,1,704,2048]{3,2,1,0:T(8,128)(2,1)}), bf16[1,1,5632,2048]{3,2,1,0:T(8,128)(2,1)}) %all-gather.17.cloned.1.call-update) | async-done | bytes 23068688 | tf_op jit(solution)/shard_map/all_gather | solution.py:71
  348.7 57.5 %fusion.10 = bf16[2048,2048]{1,0:T(8,128)(2,1)} fusion(bf16[2048,5632]{1,0:T(8,128)(2,1)} %multiply_convert_fusion.1, bf16[1,1,5632,2048]{3,2,1,0:T(8,128)(2,1)} %all-gather.17.cloned.1.call-done), kind=kOutput, calls=%fused_computation.22 | convolution fusion | flops 47248834560 | bytes 54525952 | tf_op jit(solution)/shard_map/erf,efd->erd/dot_general | solution.py:40
  406.3 5.9 all-to-all-start.1
  413.0 0.6 fusion.34
  413.6 9.1 gather_fusion.4
  422.9 1.1 reduce-window.16
  424.8 4.5 scatter_custom_fusion.1
  429.4 0.2 fusion.25
  429.9 76.6 %all-to-all-done.1 = bf16[1,4,512,2048]{3,2,0,1:T(8,128)(2,1)} async-done(((bf16[1,4,512,2048]{3,2,0,1:T(8,128)(2,1)}), bf16[1,4,512,2048]{3,2,0,1:T(8,128)(2,1)}, u32[]{:S(2)}, u32[]{:S(2)}) %all-to-all-start.1) | async-done | bytes 8388640 | tf_op jit(solution)/shard_map/all_to_all | solution.py:73
  506.5 13.4 %gather_fusion.1 = bf16[1024,2048]{1,0:T(8,128)(2,1)} fusion(bf16[2048,2048]{1,0:T(8,128)(2,1)} %bitcast.15, s32[1024]{0:T(1024)S(1)} %broadcast_clamp_fusion.1), kind=kCustom, calls=%fused_computation.3 | custom fusion | bytes 8392704 | tf_op jit(solution)/shard_map/gather | solution.py:74
  520.0 9.7 reshape.226
  529.7 14.2 %multiply_reduce_fusion.1 = f32[512,2048]{1,0:T(8,128)S(1)} fusion(f32[512,2,2048]{2,1,0:T(2,128)} %reshape.226, f32[512,2]{1,0:T(8,128)S(1)} %fusion.24), kind=kLoop, calls=%fused_computation.21 | loop fusion | flops 3145728 | bytes 12587008 | tf_op jit(solution)/shard_map/reduce_sum | solution.py:44
  543.8 0.7 fusion.20
  544.5 1.4 copy-done.6
  545.9 0.5 fusion.22
  546.5 11.0 %gather_fusion.2 = bf16[2048,2048]{1,0:T(8,128)(2,1)} fusion(bf16[512,2048]{1,0:T(8,128)(2,1)S(1)} %fusion.22, s32[2048]{0:T(1024)S(1)} %fusion.41), kind=kCustom, calls=%fused_computation.4 | custom fusion | bytes 16785408 | tf_op jit(solution)/shard_map/gather | solution.py:67
  557.4 5.7 all-to-all-start.2
  563.1 93.3 %all-to-all-done.2 = bf16[1,4,512,2048]{3,2,0,1:T(8,128)(2,1)} async-done(((bf16[1,4,512,2048]{3,2,0,1:T(8,128)(2,1)}), bf16[1,4,512,2048]{3,2,0,1:T(8,128)(2,1)}, u32[]{:S(2)}, u32[]{:S(2)}) %all-to-all-start.2) | async-done | bytes 8388640 | tf_op jit(solution)/shard_map/all_to_all | solution.py:68
  656.5 56.5 %fusion.3 = f32[2048,5632]{1,0:T(8,128)} fusion(bf16[2048,2048]{1,0:T(8,128)(2,1)} %bitcast.25, bf16[1,1,2048,5632]{2,3,1,0:T(8,128)(2,1)} %all-gather.19.cloned.1.call-done), kind=kOutput, calls=%fused_computation.13 | convolution fusion | flops 47244640256 | bytes 77594624 | tf_op jit(solution)/shard_map/erd,edf->erf/dot_general | solution.py:37
  713.0 68.8 %multiply_convert_fusion = bf16[2048,5632]{1,0:T(8,128)(2,1)} fusion(f32[2048,5632]{1,0:T(8,128)} %fusion.3, bf16[2048,2048]{1,0:T(8,128)(2,1)} %bitcast.25, bf16[1,1,2048,5632]{2,3,1,0:T(8,128)(2,1)} %all-gather.21.cloned.1.call-done), kind=kOutput, calls=%fused_computation.8 | convolution fusion | flops 47313846272 | bytes 100663296 | tf_op jit(solution)/shard_map/erd,edf->erf/dot_general | solution.py:38
  781.8 57.5 %fusion.13 = bf16[2048,2048]{1,0:T(8,128)(2,1)} fusion(bf16[2048,5632]{1,0:T(8,128)(2,1)} %multiply_convert_fusion, bf16[1,1,5632,2048]{3,2,1,0:T(8,128)(2,1)} %all-gather.23.cloned.1.call-done), kind=kOutput, calls=%fused_computation.23 | convolution fusion | flops 47248834560 | bytes 54525952 | tf_op jit(solution)/shard_map/erf,efd->erd/dot_general | solution.py:40
  839.3 6.2 all-to-all-start.3
  845.8 0.6 fusion.32
  846.5 9.1 gather_fusion.5
  855.9 0.2 fusion.27
  856.4 81.5 %all-to-all-done.3 = bf16[1,4,512,2048]{3,2,0,1:T(8,128)(2,1)} async-done(((bf16[1,4,512,2048]{3,2,0,1:T(8,128)(2,1)}), bf16[1,4,512,2048]{3,2,0,1:T(8,128)(2,1)}, u32[]{:S(2)}, u32[]{:S(2)}) %all-to-all-start.3) | async-done | bytes 8388640 | tf_op jit(solution)/shard_map/all_to_all | solution.py:73
  937.9 13.3 %gather_fusion.3 = bf16[1024,2048]{1,0:T(8,128)(2,1)} fusion(bf16[2048,2048]{1,0:T(8,128)(2,1)} %bitcast.31, s32[1024]{0:T(1024)S(1)} %broadcast_clamp_fusion), kind=kCustom, calls=%fused_computation.5 | custom fusion | bytes 8392704 | tf_op jit(solution)/shard_map/gather | solution.py:74
  951.2 9.7 reshape.227
  960.9 14.2 %multiply_reduce_fusion = f32[512,2048]{1,0:T(8,128)S(1)} fusion(f32[512,2,2048]{2,1,0:T(2,128)} %reshape.227, f32[512,2]{1,0:T(8,128)S(1)} %fusion.26), kind=kLoop, calls=%fused_computation.20 | loop fusion | flops 3145728 | bytes 12587008 | tf_op jit(solution)/shard_map/reduce_sum | solution.py:44
  975.0 2.1 fusion.23
  (97 shorter events, 4.6 us)
Async XLA Ops:
  6.5 142.9 %all-gather.13.cloned.1.call-start = ((), (), s32[]{:S(2)}) async-start(), calls=%async_computation.4 | async-start | bytes 25952256 | tf_op jit(solution)/shard_map/all_gather | solution.py:69
  12.8 224.1 %all-gather.15.cloned.1.call-start = ((), (), s32[]{:S(2)}) async-start(), calls=%async_computation.5 | async-start | bytes 25952256 | tf_op jit(solution)/shard_map/all_gather | solution.py:70
  19.2 7.7 copy-start.21
  19.2 15.1 %copy-start.4 = (bf16[512,2048]{1,0:T(8,128)(2,1)S(1)}, bf16[512,2048]{1,0:T(8,128)(2,1)}, u32[]{:S(2)}) copy-start(bf16[512,2048]{1,0:T(8,128)(2,1)} %param.9) | copy-start | bytes 6291460
  19.2 329.5 %all-gather.17.cloned.1.call-start = ((), (), s32[]{:S(2)}) async-start(), calls=%async_computation.6 | async-start | bytes 25952256 | tf_op jit(solution)/shard_map/all_gather | solution.py:71
  25.6 9.2 copy-start.20
  25.6 537.5 %all-gather.19.cloned.1.call-start = ((), (), s32[]{:S(2)}) async-start(), calls=%async_computation.7 | async-start | bytes 25952256 | tf_op jit(solution)/shard_map/all_gather | solution.py:69
  26.3 686.7 %all-gather.21.cloned.1.call-start = ((), (), s32[]{:S(2)}) async-start(), calls=%async_computation.8 | async-start | bytes 25952256 | tf_op jit(solution)/shard_map/all_gather | solution.py:70
  27.7 20.8 %copy-start.8 = (s32[1,512,2]{2,1,0:T(8,128)}, s32[1,512,2]{2,1,0:T(8,128)S(1)}, u32[]{:S(2)}) copy-start(s32[1,512,2]{2,1,0:T(8,128)S(1)} %copy.18) | copy-start | bytes 12292
  29.8 18.7 %copy-start.22 = (s32[1024]{0:T(1024)}, s32[1024]{0:T(1024)S(1)}, u32[]{:S(2)}) copy-start(s32[1024]{0:T(1024)S(1)} %add_select_fusion) | copy-start | bytes 12292
  29.9 4.8 copy-start.16
  37.5 11.0 %copy-start = (bf16[512,2048]{1,0:T(8,128)(2,1)}, bf16[512,2048]{1,0:T(8,128)(2,1)S(1)}, u32[]{:S(2)}) copy-start(bf16[512,2048]{1,0:T(8,128)(2,1)S(1)} %fusion.18) | copy-start | bytes 6291460
  48.5 100.9 %all-to-all-start = ((bf16[1,4,512,2048]{3,2,0,1:T(8,128)(2,1)}), bf16[1,4,512,2048]{3,2,0,1:T(8,128)(2,1)}, u32[]{:S(2)}, u32[]{:S(2)}) async-start(bf16[1,4,512,2048]{3,2,0,1:T(8,128)(2,1)} %bitcast.120), calls=%async_computation | async-start | bytes 16777216 | tf_op jit(solution)/shard_map/all_to_all | solution.py:68
  54.5 727.3 %all-gather.23.cloned.1.call-start = ((), (), s32[]{:S(2)}) async-start(), calls=%async_computation.9 | async-start | bytes 25952256 | tf_op jit(solution)/shard_map/all_gather | solution.py:71
  406.3 5.9 copy-start.15
  406.3 6.4 copy-start.9
  406.3 6.7 copy-start.1
  406.3 6.7 copy-start.12
  406.3 100.2 %all-to-all-start.1 = ((bf16[1,4,512,2048]{3,2,0,1:T(8,128)(2,1)}), bf16[1,4,512,2048]{3,2,0,1:T(8,128)(2,1)}, u32[]{:S(2)}, u32[]{:S(2)}) async-start(bf16[1,4,512,2048]{3,2,0,1:T(8,128)(2,1)} %bitcast.122), calls=%async_computation.1 | async-start | bytes 16777216 | tf_op jit(solution)/shard_map/all_to_all | solution.py:73
  412.3 12.1 %copy-start.10 = (s32[1,512,2]{2,1,0:T(8,128)}, s32[1,512,2]{2,1,0:T(8,128)S(1)}, u32[]{:S(2)}) copy-start(s32[1,512,2]{2,1,0:T(8,128)S(1)} %copy.19) | copy-start | bytes 12292
  413.6 16.1 %copy-start.17 = (s32[1024,1]{0,1:T(1,128)S(1)}, s32[1024,1]{0,1:T(1,128)}, u32[]{:S(2)}) copy-start(s32[1024,1]{0,1:T(1,128)} %copy-done.16) | copy-start | bytes 12292
  424.8 95.2 %copy-start.18 = (s32[1024,1]{0,1:T(1,128)}, s32[1024,1]{0,1:T(1,128)S(1)}, u32[]{:S(2)}) copy-start(s32[1024,1]{0,1:T(1,128)S(1)} %compare_select_fusion.2) | copy-start | bytes 12292
  529.6 14.2 %copy-start.5 = (bf16[512,2048]{1,0:T(8,128)(2,1)S(1)}, bf16[512,2048]{1,0:T(8,128)(2,1)}, u32[]{:S(2)}) copy-start(bf16[512,2048]{1,0:T(8,128)(2,1)} %param.9) | copy-start | bytes 6291460
  529.7 16.3 %copy-start.14 = (f32[1,2048]{1,0:T(1,128)S(1)}, f32[1,2048]{1,0:T(1,128)}, u32[]{:S(2)}) copy-start(f32[1,2048]{1,0:T(1,128)} %get-tuple-element.14) | copy-start | bytes 24580
  544.5 1.4 copy-start.6
  546.5 11.0 %copy-start.2 = (bf16[512,2048]{1,0:T(8,128)(2,1)}, bf16[512,2048]{1,0:T(8,128)(2,1)S(1)}, u32[]{:S(2)}) copy-start(bf16[512,2048]{1,0:T(8,128)(2,1)S(1)} %fusion.22) | copy-start | bytes 6291460
  557.4 99.1 %all-to-all-start.2 = ((bf16[1,4,512,2048]{3,2,0,1:T(8,128)(2,1)}), bf16[1,4,512,2048]{3,2,0,1:T(8,128)(2,1)}, u32[]{:S(2)}, u32[]{:S(2)}) async-start(bf16[1,4,512,2048]{3,2,0,1:T(8,128)(2,1)} %bitcast.121), calls=%async_computation.2 | async-start | bytes 16777216 | tf_op jit(solution)/shard_map/all_to_all | solution.py:68
  839.3 6.2 copy-start.11
  839.3 6.5 copy-start.19
  839.3 6.5 copy-start.3
  839.3 6.5 copy-start.13
  839.3 98.6 %all-to-all-start.3 = ((bf16[1,4,512,2048]{3,2,0,1:T(8,128)(2,1)}), bf16[1,4,512,2048]{3,2,0,1:T(8,128)(2,1)}, u32[]{:S(2)}, u32[]{:S(2)}) async-start(bf16[1,4,512,2048]{3,2,0,1:T(8,128)(2,1)} %bitcast.123), calls=%async_computation.3 | async-start | bytes 16777216 | tf_op jit(solution)/shard_map/all_to_all | solution.py:73
  960.9 14.2 %copy-start.7 = (bf16[512,2048]{1,0:T(8,128)(2,1)S(1)}, bf16[512,2048]{1,0:T(8,128)(2,1)}, u32[]{:S(2)}) copy-start(bf16[512,2048]{1,0:T(8,128)(2,1)} %copy-done.6) | copy-start | bytes 6291460
Sparse Core Ops, SparseCore 0:
  13.0 112.2 all-gather.12
  126.8 110.1 all-gather.14
  238.6 110.1 all-gather.16
  350.2 110.1 all-gather.18
  461.8 110.1 all-gather.20
  573.4 110.1 all-gather.22
where the time goes:
time: 993 us; the launch traced here: 984 us
  waiting for transfers between devices  422 us (42%)
  matrix products  367 us (37%)
  local copies, waits for them, and re-layouts  119 us (12%)
  other arithmetic  38.6 us (4%)
  starting transfers between devices  23.9 us (2%)
  between operations  14.5 us (1%)
    all_to_all x2, waiting for transfers between devices, device_step(): recv_buf = lax.all_to_all(send_buf, 'ep', 1, 1, tiled=True)  188 us
    all_to_all x2, waiting for transfers between devices, device_step(): lax.all_to_all(expert_out.reshape(n_local, owners, capacity, d_model), 'e...  158 us
    dot_general x2, matrix products, expert_ffn(): jnp.einsum('erd,edf->erf', expert_rows, up_full, preferred_element_type=j...  138 us
    dot_general x2, matrix products, expert_ffn(): jnp.einsum('erf,efd->erd', inner_act, down_full, preferred_element_type=j...  115 us
    dot_general x2, matrix products, expert_ffn(): jnp.einsum('erd,edf->erf', expert_rows, gate_full, preferred_element_type...  113 us
    all_gather x2, waiting for transfers between devices, device_step(): down_full = lax.all_gather(down_w[layer_idx], 'fsdp', axis=1, tiled=True)  43 us
    all_gather x2, waiting for transfers between devices, device_step(): up_full = lax.all_gather(up_w[layer_idx], 'fsdp', axis=2, tiled=True)  31.1 us
    reduce_sum x2, other arithmetic, combine(): jnp.sum(gate_probs[..., None] * pair_out.astype(jnp.float32), axis=-2)  28.3 us
  transfers between devices with their start and end apart: 10, of which 6 were waited for; matrix products, arithmetic and copies ran while one was open for 43% of the time, Pallas kernels for 0%

commit v1 on v0

v1 whole, which is shorter than its diff:
```python
import functools

import jax
import jax.numpy as jnp
from jax import lax
from jax.experimental import pallas as pl
from jax.experimental.pallas import tpu as pltpu
from jax.sharding import PartitionSpec as P

MESH = pl.DeviceIdType.MESH
NORM_EPS = 1e-5
CHUNK = 128


def kernel(n_ep, n_fs, x_hbm, norm_ref, router_ref, w1, w3, w2, routes_ref,
           out_hbm, g1, g3, g2, h_land, o_land, r_land,
           h_all, acc, b1, b3, b2, act, xs, orecv, gates,
           ws, wr, hs, hr, os_, or_, ld):
    layers, tok_dev = routes_ref.shape[0], routes_ref.shape[1]
    d_model = x_hbm.shape[1]
    chips = n_fs // 2
    y = lax.axis_index("ep")
    f = lax.axis_index("fsdp")
    xc = f // 2
    core = lax.rem(f, 2)

    def fs_index(dx, dk):
        return lax.rem(xc + dx, chips) * 2 + lax.rem(core + dk, 2)

    right, left, opp, partner = fs_index(1, 0), fs_index(chips - 1, 0), fs_index(2, 0), fs_index(0, 1)
    up, down = lax.rem(y + 1, n_ep), lax.rem(y + n_ep - 1, n_ep)
    to_right, to_left, to_partner = {"fsdp": right}, {"fsdp": left}, {"fsdp": partner}
    to_up, to_down = {"ep": up}, {"ep": down}

    own_refs, land_refs, bufs = (w1, w3, w2), (g1, g3, g2), (b1, b3, b2)

    class Lazy:
        def __init__(self, *args):
            self.args = args

        def start(self):
            remote(*self.args).start()

        def wait_send(self):
            remote(*self.args).wait_send()

    def remote(src, dst, send, recv, dev):
        return pltpu.make_async_remote_copy(src_ref=src, dst_ref=dst, send_sem=send, recv_sem=recv,
                                            device_id=dev, device_id_type=MESH)

    def own(l, t):
        return own_refs[t].at[l, 0]

    def land(l, t, slot):
        return land_refs[t].at[l, slot]

    def half(ref, i):
        rows = ref.shape[0] // 2
        return ref.at[pl.ds(i * rows, rows)]

    def weight_copies(l, t):
        return (
            Lazy(own(l, t), land(l, t, f), ws.at[l, t, 0], wr.at[l, t, 2], to_right),
            Lazy(own(l, t), land(l, t, f), ws.at[l, t, 1], wr.at[l, t, 3], to_left),
            Lazy(own(l, t), land(l, t, f), ws.at[l, t, 2], wr.at[l, t, 1], to_partner),
            Lazy(half(land(l, t, left), 0), half(land(l, t, left), 0), ws.at[l, t, 3], wr.at[l, t, 6], to_right),
            Lazy(half(land(l, t, right), 1), half(land(l, t, right), 1), ws.at[l, t, 4], wr.at[l, t, 8], to_left),
            Lazy(land(l, t, left), land(l, t, left), ws.at[l, t, 5], wr.at[l, t, 4], to_partner),
            Lazy(land(l, t, right), land(l, t, right), ws.at[l, t, 6], wr.at[l, t, 5], to_partner),
            Lazy(half(land(l, t, opp), 0), half(land(l, t, opp), 0), ws.at[l, t, 7], wr.at[l, t, 7], to_partner),
            Lazy(half(land(l, t, opp), 1), half(land(l, t, opp), 1), ws.at[l, t, 8], wr.at[l, t, 9], to_partner),
        )

    def wait_weight(l, t, slot, sem):
        ref = land(l, t, slot)
        remote(ref, ref, ws.at[l, t, 0], wr.at[l, t, sem], to_partner).wait_recv()

    def wait_weight_half(l, t, slot, i, sem):
        ref = half(land(l, t, slot), i)
        remote(ref, ref, ws.at[l, t, 0], wr.at[l, t, sem], to_partner).wait_recv()

    def push_own(l, t):
        for copy in weight_copies(l, t)[:3]:
            copy.start()

    def pass_sides(l, t):
        wait_weight(l, t, left, 2)
        wait_weight(l, t, right, 3)
        for copy in weight_copies(l, t)[3:7]:
            copy.start()

    def pass_opp(l, t):
        wait_weight_half(l, t, opp, 0, 6)
        wait_weight_half(l, t, opp, 1, 8)
        for copy in weight_copies(l, t)[7:9]:
            copy.start()

    def slot_of(s):
        c = s // 2
        dx = jnp.minimum(c, 1) * (lax.rem(c + 1, 3) + 1)
        return fs_index(dx, lax.rem(s, 2))

    def load(l, t, s):
        @pl.when(s == 1)
        def _():
            wait_weight(l, t, partner, 1)

        @pl.when(s == 3)
        def _():
            wait_weight(l, t, fs_index(chips - 1, 1), 4)

        @pl.when(s == 5)
        def _():
            wait_weight(l, t, fs_index(1, 1), 5)

        @pl.when(s == 6)
        def _():
            pass_opp(l, t)

        @pl.when(s == 7)
        def _():
            wait_weight_half(l, t, fs_index(2, 1), 0, 7)
            wait_weight_half(l, t, fs_index(2, 1), 1, 9)

        @pl.when(s == 0)
        def _():
            pltpu.make_async_copy(own(l, t), bufs[t], ld.at[t]).start()

        @pl.when(s > 0)
        def _():
            pltpu.make_async_copy(land(l, t, slot_of(s)), bufs[t], ld.at[t]).start()

    def load_wait(t):
        pltpu.make_async_copy(own(0, t), bufs[t], ld.at[t]).wait()

    barrier = pltpu.get_barrier_semaphore()
    for dev in (to_right, to_left, to_partner, to_up, to_down):
        pl.semaphore_signal(barrier, inc=1, device_id=dev, device_id_type=MESH)
    pl.semaphore_wait(barrier, 5)

    x_copy = pltpu.make_async_copy(x_hbm, xs, ld.at[3])
    x_copy.start()
    for t in range(3):
        push_own(0, t)
    x_copy.wait()

    def normalise(l):
        def step(i, carry):
            rows = pl.ds(pl.multiple_of(i * CHUNK, CHUNK), CHUNK)
            wide = xs[rows, :].astype(jnp.float32)
            inv = lax.rsqrt(jnp.mean(wide * wide, axis=-1, keepdims=True) + NORM_EPS)
            hidden = (wide * inv * norm_ref[l]).astype(jnp.bfloat16)
            h_all[0, rows, :] = hidden
            logits = jnp.dot(hidden, router_ref[l], preferred_element_type=jnp.float32)
            lane = lax.broadcasted_iota(jnp.int32, logits.shape, 1)
            ids = routes_ref[l, rows, :]
            pick0 = jnp.sum(jnp.where(lane == ids[:, 0:1], logits, 0.0), axis=-1, keepdims=True)
            pick1 = jnp.sum(jnp.where(lane == ids[:, 1:2], logits, 0.0), axis=-1, keepdims=True)
            top = jnp.maximum(pick0, pick1)
            e0, e1 = jnp.exp(pick0 - top), jnp.exp(pick1 - top)
            total = e0 + e1
            gates[rows, :] = jnp.where(lane == 0, e0 / total, e1 / total)
            return carry
        lax.fori_loop(0, tok_dev // CHUNK, step, 0)

    def hidden_copies(l):
        return (
            Lazy(h_all.at[0], h_land.at[l, 0], hs.at[l, 0], hr.at[l, 0], to_up),
            Lazy(h_all.at[0], h_land.at[l, 1], hs.at[l, 1], hr.at[l, 1], to_down),
            Lazy(half(h_land.at[l, 0], 0), half(h_land.at[l, 2], 0), hs.at[l, 2], hr.at[l, 2], to_up),
            Lazy(half(h_land.at[l, 1], 1), half(h_land.at[l, 2], 1), hs.at[l, 3], hr.at[l, 3], to_down),
        )

    def send_hidden(l):
        for copy in hidden_copies(l)[:2]:
            copy.start()

    def take_hidden(l, between):
        copies = hidden_copies(l)
        for i in (0, 1):
            remote(h_land.at[l, i], h_land.at[l, i], hs.at[l, i], hr.at[l, i], to_up).wait_recv()
            copies[2 + i].start()
            pltpu.make_async_copy(h_land.at[l, i], h_all.at[1 + i], ld.at[4 + i]).start()
        between()
        for i in (0, 1):
            ref = half(h_land.at[l, 2], i)
            remote(ref, ref, hs.at[l, 2 + i], hr.at[l, 2 + i], to_up).wait_recv()
        pltpu.make_async_copy(h_land.at[l, 2], h_all.at[3], ld.at[6]).start()
        for i in range(3):
            pltpu.make_async_copy(h_land.at[l, i], h_all.at[1 + i], ld.at[4 + i]).wait()
        for copy in copies:
            copy.wait_send()

    def clear_acc():
        def step(i, carry):
            rows = pl.ds(pl.multiple_of(lax.rem(i, 4) * CHUNK, CHUNK), CHUNK)
            acc[i // 4, rows, :] = jnp.zeros((CHUNK, d_model), jnp.float32)
            return carry
        lax.fori_loop(0, 4 * (tok_dev // CHUNK), step, 0)

    def experts(l):
        def slice_step(s, carry):
            load_wait(0)
            load_wait(1)

            def gate_up(rb, c):
                @pl.when(rb == 2)
                def _():
                    if l == 0:
                        @pl.when(s == 2)
                        def _():
                            pass_sides(l, 2)
                    load(l, 2, s)
                    if l == 0:
                        @pl.when(s == 4)
                        def _():
                            for t in range(3):
                                push_own(1, t)
                u = jnp.dot(h_all[rb], b1[...], preferred_element_type=jnp.float32)
                v = jnp.dot(h_all[rb], b3[...], preferred_element_type=jnp.float32)
                act[rb] = (u * jax.nn.sigmoid(u) * v).astype(jnp.bfloat16)
                return c
            lax.fori_loop(0, 4, gate_up, 0)

            if l == 0:
                @pl.when(s == 1)
                def _():
                    pass_sides(l, 0)
                    pass_sides(l, 1)

            @pl.when(s < 7)
            def _():
                load(l, 0, s + 1)
                load(l, 1, s + 1)
            load_wait(2)

            def down_proj(rb, c):
                cols = 512
                for n in range(d_model // cols):
                    part = pl.ds(n * cols, cols)
                    acc[rb, :, part] += jnp.dot(act[rb], b2[:, part], preferred_element_type=jnp.float32)
                return c
            lax.fori_loop(0, 4, down_proj, 0)
            return carry

        load(l, 0, 0)
        load(l, 1, 0)
        lax.fori_loop(0, 8, slice_step, 0)

    def round_block(block):
        def step(i, carry):
            rows = pl.ds(pl.multiple_of(i * CHUNK, CHUNK), CHUNK)
            h_all[block, rows, :] = acc[block, rows, :].astype(jnp.bfloat16)
            return carry
        lax.fori_loop(0, tok_dev // CHUNK, step, 0)

    def output_copies(l):
        return (
            Lazy(half(h_all.at[3], 0), r_land.at[l, 0], os_.at[l, 0], or_.at[l, 0], to_up),
            Lazy(half(h_all.at[3], 1), r_land.at[l, 1], os_.at[l, 1], or_.at[l, 1], to_down),
            Lazy(h_all.at[1], o_land.at[l, 0], os_.at[l, 2], or_.at[l, 2], to_down),
            Lazy(h_all.at[2], o_land.at[l, 1], os_.at[l, 3], or_.at[l, 3], to_up),
            Lazy(r_land.at[l, 0], half(o_land.at[l, 2], 0), os_.at[l, 4], or_.at[l, 4], to_up),
            Lazy(r_land.at[l, 1], half(o_land.at[l, 2], 1), os_.at[l, 5], or_.at[l, 5], to_down),
        )

    def return_outputs(l):
        copies = output_copies(l)
        round_block(3)
        copies[0].start()
        copies[1].start()
        round_block(1)
        copies[2].start()
        round_block(2)
        copies[3].start()
        for i in (0, 1):
            ref = r_land.at[l, i]
            remote(ref, ref, os_.at[l, i], or_.at[l, i], to_up).wait_recv()
            copies[4 + i].start()
        for i in (0, 1):
            ref = o_land.at[l, i]
            remote(ref, ref, os_.at[l, i], or_.at[l, 2 + i], to_up).wait_recv()
            pltpu.make_async_copy(ref, orecv.at[i], ld.at[4 + i]).start()
        for i in (0, 1):
            ref = half(o_land.at[l, 2], i)
            remote(ref, ref, os_.at[l, i], or_.at[l, 4 + i], to_up).wait_recv()
        pltpu.make_async_copy(o_land.at[l, 2], orecv.at[2], ld.at[6]).start()
        for i in range(3):
            pltpu.make_async_copy(o_land.at[l, i], orecv.at[i], ld.at[4 + i]).wait()
        for copy in copies:
            copy.wait_send()

    def combine(l):
        sources = (up, down, lax.rem(y + 2, n_ep))

        def step(i, carry):
            rows = pl.ds(pl.multiple_of(i * CHUNK, CHUNK), CHUNK)
            ids, gate = routes_ref[l, rows, :], gates[rows, :]
            id0, id1, gate0, gate1 = ids[:, 0:1], ids[:, 1:2], gate[:, 0:1], gate[:, 1:2]

            def term(expert, value):
                is0, is1 = id0 == expert, id1 == expert
                weight = jnp.where(is0, gate0, gate1)
                return jnp.where(jnp.logical_or(is0, is1), weight * value.astype(jnp.float32), 0.0)
            mixed = term(y, acc[0, rows, :].astype(jnp.bfloat16))
            for j, expert in enumerate(sources):
                mixed += term(expert, orecv[j, rows, :])
            xs[rows, :] = (xs[rows, :].astype(jnp.float32) + mixed).astype(jnp.bfloat16)
            return carry
        lax.fori_loop(0, tok_dev // CHUNK, step, 0)

    normalise(0)
    send_hidden(0)
    clear_acc()
    take_hidden(0, lambda: None)
    experts(0)
    return_outputs(0)
    combine(0)
    normalise(1)
    send_hidden(1)
    clear_acc()
    pass_sides(1, 0)
    take_hidden(1, lambda: pass_sides(1, 1))
    pass_sides(1, 2)
    experts(1)
    return_outputs(1)
    combine(1)
    out_copy = pltpu.make_async_copy(xs, out_hbm, ld.at[3])
    out_copy.start()
    for l in range(layers):
        for t in range(3):
            for copy in weight_copies(l, t):
                copy.wait_send()
    out_copy.wait()


def solution(mesh):
    n_ep, n_fs = mesh.shape["ep"], mesh.shape["fsdp"]
    token_spec = P(("rep", "ep", "fsdp"), None)
    expert_in_spec = P(None, "ep", None, "fsdp")
    expert_out_spec = P(None, "ep", "fsdp", None)
    route_spec = P(None, ("rep", "ep", "fsdp"), None)

    def device_step(x_in, norm_w, router_w, gate_w, up_w, down_w, routes):
        layers, tok_dev, top_k = routes.shape
        d_model = x_in.shape[1]
        ff = gate_w.shape[3]
        router_pad = jnp.pad(router_w, ((0, 0), (0, 0), (0, 128 - router_w.shape[2])))
        bf16 = jnp.bfloat16
        hbm, vmem = pl.BlockSpec(memory_space=pl.ANY), pl.BlockSpec(memory_space=pltpu.VMEM)
        shape = jax.ShapeDtypeStruct
        outs = pl.pallas_call(
            functools.partial(kernel, n_ep, n_fs),
            name="moe_layers",
            out_shape=(shape((tok_dev, d_model), bf16),
                       shape((layers, n_fs, d_model, ff), bf16),
                       shape((layers, n_fs, d_model, ff), bf16),
                       shape((layers, n_fs, ff, d_model), bf16),
                       shape((layers, 3, tok_dev, d_model), bf16),
                       shape((layers, 3, tok_dev, d_model), bf16),
                       shape((layers, 2, tok_dev // 2, d_model), bf16)),
            in_specs=[hbm, vmem, vmem, hbm, hbm, hbm, vmem],
            out_specs=(hbm,) * 7,
            scratch_shapes=[
                pltpu.VMEM((4, tok_dev, d_model), bf16),
                pltpu.VMEM((4, tok_dev, d_model), jnp.float32),
                pltpu.VMEM((d_model, ff), bf16),
                pltpu.VMEM((d_model, ff), bf16),
                pltpu.VMEM((ff, d_model), bf16),
                pltpu.VMEM((4, tok_dev, ff), bf16),
                pltpu.VMEM((tok_dev, d_model), bf16),
                pltpu.VMEM((3, tok_dev, d_model), bf16),
                pltpu.VMEM((tok_dev, 128), jnp.float32),
                pltpu.SemaphoreType.DMA((layers, 3, 9)),
                pltpu.SemaphoreType.DMA((layers, 3, 10)),
                pltpu.SemaphoreType.DMA((layers, 4)),
                pltpu.SemaphoreType.DMA((layers, 4)),
                pltpu.SemaphoreType.DMA((layers, 6)),
                pltpu.SemaphoreType.DMA((layers, 6)),
                pltpu.SemaphoreType.DMA((7,)),
            ],
            compiler_params=pltpu.CompilerParams(collective_id=0, has_side_effects=True,
                                                 vmem_limit_bytes=66_000_000),
        )(x_in, norm_w[:, None, :], router_pad, gate_w, up_w, down_w, routes)
        return outs[0]

    return jax.shard_map(device_step, mesh=mesh,
                         in_specs=(token_spec, P(), P(), expert_in_spec, expert_in_spec, expert_out_spec, route_spec),
                         out_specs=token_spec, check_vma=False)
```

time: 993 us -> 801 us (0.81)
  Pallas kernels: 0 us -> 774 us
  waiting for transfers between devices: 422 us -> 0 us
  matrix products: 367 us -> 0 us
  local copies, waits for them, and re-layouts: 119 us -> 25.7 us
  other arithmetic: 38.6 us -> 0 us
  starting transfers between devices: 23.9 us -> 0 us
  between operations: 14.5 us -> 0.01 us
    pallas_call x0 -> x1, Pallas kernels: none -> 774 us  [device_step(): pl.pallas_call(functools.partial(kernel, n_ep, n_fs), name='moe_layers',...]
    dot_general x8 -> x0, matrix products: 367 us -> none  [the longest x2 138 us: expert_ffn(): jnp.einsum('erd,edf->erf', expert_rows, up_full, preferred_element_type=j...]
    all_to_all x4 -> x0, waiting for transfers between devices: 346 us -> none  [the longest x2 188 us: device_step(): recv_buf = lax.all_to_all(send_buf, 'ep', 1, 1, tiled=True)]
    all_gather x6 -> x0, waiting for transfers between devices: 74.1 us -> none  [the longest x2 43 us: device_step(): down_full = lax.all_gather(down_w[layer_idx], 'fsdp', axis=1, tiled=True)]
    gather x10 -> x0, local copies, waits for them, and re-layouts: 67.5 us -> none  [the longest x2 26.7 us: device_step(): back_buf.reshape(experts * capacity, d_model)[pair_slot]]
    reduce_sum x8 -> x0, other arithmetic: 30 us -> none  [the longest x2 28.3 us: combine(): jnp.sum(gate_probs[..., None] * pair_out.astype(jnp.float32), axis=-2)]
    all_to_all x4 -> x0, starting transfers between devices: 23.7 us -> none  [the longest x2 12.1 us: device_step(): lax.all_to_all(expert_out.reshape(n_local, owners, capacity, d_model), 'e...]
    unnamed x48 -> x5, local copies, waits for them, and re-layouts: 1.76 us -> 23.2 us
  transfers between devices with their start and end apart: 10 -> 0, of which waited for: 6 -> 0; matrix products, arithmetic and copies ran while one was open for 43% -> 0% of each run, Pallas kernels for 0% -> 0%
where the time goes in v1:
time: 801 us; the launch traced here: 800 us
  Pallas kernels  774 us (97%)
  local copies, waits for them, and re-layouts  25.7 us (3%)
    pallas_call x1, Pallas kernels, device_step(): pl.pallas_call(functools.partial(kernel, n_ep, n_fs), name='moe_layers',...  774 us
    unnamed x5, local copies, waits for them, and re-layouts  23.2 us

profile of v1, /device:TPU:98, one launch (start us, length us, event | category | flops | bytes accessed | tf_op | source)
XLA Modules:
  0.0 799.6 jit_solution(4540482671957777762)
XLA Ops:
  0.0 1.3 broadcast_in_dim.3.norm_ref
  1.3 1.7 copy.11.routes_ref
  3.1 1.3 copy.8
  4.3 1.2 pad.4.router_ref
  5.5 8.5 %copy.9.w1 = bf16[2,1,2048,704]{3,2,1,0:T(8,128)(2,1)} copy(bf16[2,1,2048,704]{2,3,1,0:T(8,128)(2,1)} %param.10) | data formatting | bytes 11534336 | tf_op args[3]
  14.0 8.5 %copy.10.w3 = bf16[2,1,2048,704]{3,2,1,0:T(8,128)(2,1)} copy(bf16[2,1,2048,704]{2,3,1,0:T(8,128)(2,1)} %param.11) | data formatting | bytes 11534336 | tf_op args[4]
  22.6 773.8 %moe_layers.1 = (bf16[512,2048]{1,0:T(8,128)(2,1)}, bf16[2,8,2048,704]{3,2,1,0:T(8,128)(2,1)}, bf16[2,8,2048,704]{3,2,1,0:T(8,128)(2,1)}, bf16[2,8,704,2048]{3,2...) custom-call(bf16[512,2048]{1,0:T(8,128)(2,1)} %x_hbm.1, ...), custom_call_target="tpu_custom_call" | custom-call | tf_op jit(solution)/shard_map/moe_layers/pallas_call | solution.py:352
  796.4 3.2 copy.13

commit v2 on v0

v2 whole, which is shorter than its diff:
```python
import functools

import jax
import jax.numpy as jnp
from jax import lax
from jax.experimental import pallas as pl
from jax.experimental.pallas import tpu as pltpu
from jax.sharding import PartitionSpec as P

MESH = pl.DeviceIdType.MESH
NORM_EPS = 1e-5
NT = (((1,), (1,)), ((), ()))
CHUNK = 128


def kernel(n_ep, n_fs, x_hbm, norm_ref, router_ref, w1, w3, w2, routes_ref,
           out_hbm, g1, g3, g2, h_land, o_land, r_land,
           h_all, acc, b13, b2, act, xs, orecv, gates,
           ws, wr, hs, hr, os_, or_, ld):
    layers, tok_dev = routes_ref.shape[0], routes_ref.shape[1]
    d_model, ff = x_hbm.shape[1], w2.shape[2]
    part = tok_dev // 2
    chips = n_fs // 2
    y = lax.axis_index("ep")
    f = lax.axis_index("fsdp")
    xc = f // 2
    core = lax.rem(f, 2)

    def ring_slot(r, k):
        return lax.rem(xc + (1 - k) * (chips - r) + k * r, chips) * 2 + k

    def slot_of(s):
        return ring_slot(s // 2, lax.rem(core + lax.rem(s, 2), 2))

    following, previous, partner = ring_slot(chips - 1, core), ring_slot(1, core), xc * 2 + 1 - core
    up, down = lax.rem(y + 1, n_ep), lax.rem(y + n_ep - 1, n_ep)
    to_next, to_prev, to_partner = {"fsdp": following}, {"fsdp": previous}, {"fsdp": partner}
    to_up, to_down = {"ep": up}, {"ep": down}

    def remote(src, dst, send, recv, dev):
        return pltpu.make_async_remote_copy(src_ref=src, dst_ref=dst, send_sem=send, recv_sem=recv,
                                            device_id=dev, device_id_type=MESH)

    own_refs, land_refs = (w1, w3, w2), (g1, g3, g2)

    def land(l, t, slot):
        return land_refs[t].at[l, slot]

    def source(l, t, r):
        return own_refs[t].at[l, 0] if r == 0 else land(l, t, slot_of(2 * r))

    def ring_send(l, t, r):
        return remote(source(l, t, r), land(l, t, slot_of(2 * r)), ws.at[l, t, r], wr.at[l, t, 2 * r + 2], to_next)

    def partner_send(l, t, r):
        return remote(source(l, t, r), land(l, t, slot_of(2 * r)), ws.at[l, t, 3 + r], wr.at[l, t, 2 * r + 1],
                      to_partner)

    def arrived(l, t, s):
        ref = land(l, t, slot_of(s))
        remote(ref, ref, ws.at[l, t, 0], wr.at[l, t, s], to_partner).wait_recv()

    def push_own(l, t):
        ring_send(l, t, 0).start()
        partner_send(l, t, 0).start()

    def pass_ring(l, t, r):
        arrived(l, t, 2 * r)
        if r < 3:
            ring_send(l, t, r).start()
        partner_send(l, t, r).start()

    main = ff // 128 * 128
    tail = ff - main
    groups = [(c, min(256, main - c)) for c in range(0, main, 256)] + [(main, tail)]

    def load13(l, s, i):
        def start(refs):
            for c, width in groups:
                for k in (0, 1):
                    pltpu.make_async_copy(refs[k].at[pl.ds(c, width)],
                                          b13.at[lax.rem(i, 2), pl.ds(2 * c + k * width, width)], ld.at[0]).start()

        @pl.when(s == 0)
        def _():
            start((w1.at[l, 0], w3.at[l, 0]))

        @pl.when(s > 0)
        def _():
            start((land(l, 0, slot_of(s)), land(l, 1, slot_of(s))))

    def load13_wait():
        pltpu.make_async_copy(b13.at[0], b13.at[0], ld.at[0]).wait()

    def load2(l, s):
        @pl.when(s == 0)
        def _():
            pltpu.make_async_copy(w2.at[l, 0], b2, ld.at[1]).start()

        @pl.when(s > 0)
        def _():
            pltpu.make_async_copy(g2.at[l, slot_of(s)], b2, ld.at[1]).start()

    def load2_wait():
        pltpu.make_async_copy(g2.at[0, 0], b2, ld.at[1]).wait()

    def place(block, q):
        return h_all.at[2 * q + block // 2, pl.ds(block % 2 * part, part)]

    def normalise(l, q):
        def step(i, carry):
            rows = pl.ds(pl.multiple_of(q * part + i * CHUNK, CHUNK), CHUNK)
            wide = xs[rows, :].astype(jnp.float32)
            inv = lax.rsqrt(jnp.mean(wide * wide, axis=-1, keepdims=True) + NORM_EPS)
            hidden = (wide * inv * norm_ref[l:l + 1, :]).astype(jnp.bfloat16)
            h_all[2 * q, pl.ds(pl.multiple_of(i * CHUNK, CHUNK), CHUNK), :] = hidden
            logits = lax.dot_general(hidden, router_ref[l], NT, preferred_element_type=jnp.float32)
            lane = lax.broadcasted_iota(jnp.int32, logits.shape, 1)
            ids = routes_ref[l, rows, :]
            pick0 = jnp.sum(jnp.where(lane == ids[:, 0:1], logits, 0.0), axis=-1, keepdims=True)
            pick1 = jnp.sum(jnp.where(lane == ids[:, 1:2], logits, 0.0), axis=-1, keepdims=True)
            top = jnp.maximum(pick0, pick1)
            e0, e1 = jnp.exp(pick0 - top), jnp.exp(pick1 - top)
            total = e0 + e1
            gates[rows, :] = jnp.where(lax.broadcasted_iota(jnp.int32, (CHUNK, 128), 1) == 0, e0 / total, e1 / total)
            return carry
        lax.fori_loop(0, part // CHUNK, step, 0)

    def half(ref, i):
        rows = ref.shape[0] // 2
        return ref.at[pl.ds(i * rows, rows)]

    def send_side(l, q, i):
        return remote(place(0, q), h_land.at[l, q, i], hs.at[l, q, i], hr.at[l, q, i], (to_up, to_down)[i])

    def send_far(l, q, i):
        return remote(half(h_land.at[l, q, i], i), half(h_land.at[l, q, 2], i), hs.at[l, q, 2 + i],
                      hr.at[l, q, 2 + i], (to_up, to_down)[i])

    def send_hidden(l, q):
        for i in (0, 1):
            send_side(l, q, i).start()

    def hidden_load(l, q, i):
        return pltpu.make_async_copy(h_land.at[l, q, i], place(1 + i, q), ld.at[4 + i])

    def take_sides(l, q):
        for i in (0, 1):
            ref = h_land.at[l, q, i]
            remote(ref, ref, hs.at[l, q, i], hr.at[l, q, i], to_up).wait_recv()
            send_far(l, q, i).start()

    def load_sides(l, q):
        if l > 0:
            for i in range(4):
                output_copy(l - 1, q, i).wait_send()
        for i in (0, 1):
            hidden_load(l, q, i).start()
        for i in (0, 1):
            hidden_load(l, q, i).wait()

    def take_far(l, q):
        for i in (0, 1):
            ref = half(h_land.at[l, q, 2], i)
            remote(ref, ref, hs.at[l, q, 2 + i], hr.at[l, q, 2 + i], to_up).wait_recv()
        hidden_load(l, q, 2).start()
        hidden_load(l, q, 2).wait()

    def clear_acc(q):
        def step(i, carry):
            rows = pl.ds(pl.multiple_of(lax.rem(i, 4) * CHUNK, CHUNK), CHUNK)
            acc[2 * q + i // 4, rows, :] = jnp.zeros((CHUNK, d_model), jnp.float32)
            return carry
        lax.fori_loop(0, 2 * (tok_dev // CHUNK), step, 0)

    def output_copy(l, q, i):
        dev = (to_up, to_down, to_down, to_up, to_up, to_down)[i]
        far = o_land.at[l, q, 2]
        src = (half(place(3, q), 0), half(place(3, q), 1), place(1, q), place(2, q),
               r_land.at[l, q, 0], r_land.at[l, q, 1])[i]
        dst = (r_land.at[l, q, 0], r_land.at[l, q, 1], o_land.at[l, q, 0], o_land.at[l, q, 1],
               half(far, 0), half(far, 1))[i]
        return remote(src, dst, os_.at[l, q, i], or_.at[l, q, i], dev)

    def round_block(block, q):
        for i in range(part // CHUNK):
            rows = pl.ds(block % 2 * part + i * CHUNK, CHUNK)
            h_all[2 * q + block // 2, rows, :] = acc[2 * q + block // 2, rows, :].astype(jnp.bfloat16)

    def issue_outputs(l, q):
        round_block(3, q)
        output_copy(l, q, 0).start()
        output_copy(l, q, 1).start()
        round_block(1, q)
        output_copy(l, q, 2).start()
        round_block(2, q)
        output_copy(l, q, 3).start()

    def relay(l, q):
        for i in (0, 1):
            ref = r_land.at[l, q, i]
            remote(ref, ref, os_.at[l, q, i], or_.at[l, q, i], to_up).wait_recv()
            output_copy(l, q, 4 + i).start()

    def collect(l, q):
        def fetch(i):
            return pltpu.make_async_copy(o_land.at[l, q, i], orecv.at[i], ld.at[4 + i])
        for i in (0, 1):
            ref = o_land.at[l, q, i]
            remote(ref, ref, os_.at[l, q, i], or_.at[l, q, 2 + i], to_up).wait_recv()
            fetch(i).start()
        for i in (0, 1):
            ref = half(o_land.at[l, q, 2], i)
            remote(ref, ref, os_.at[l, q, i], or_.at[l, q, 4 + i], to_up).wait_recv()
        fetch(2).start()
        for i in range(3):
            fetch(i).wait()

    def combine(l, q):
        collect(l, q)
        sources = (up, down, lax.rem(y + 2, n_ep))

        def step(i, carry):
            local = pl.ds(pl.multiple_of(i * CHUNK, CHUNK), CHUNK)
            rows = pl.ds(pl.multiple_of(q * part + i * CHUNK, CHUNK), CHUNK)
            ids, gate = routes_ref[l, rows, :], gates[rows, :]
            id0, id1, gate0, gate1 = ids[:, 0:1], ids[:, 1:2], gate[:, 0:1], gate[:, 1:2]

            def term(expert, value):
                is0, is1 = id0 == expert, id1 == expert
                weight = jnp.where(is0, gate0, gate1)
                return jnp.where(jnp.logical_or(is0, is1), weight * value.astype(jnp.float32), 0.0)
            mixed = term(y, acc[2 * q, local, :].astype(jnp.bfloat16))
            for j, expert in enumerate(sources):
                mixed += term(expert, orecv[j, local, :])
            xs[rows, :] = (xs[rows, :].astype(jnp.float32) + mixed).astype(jnp.bfloat16)
            return carry
        lax.fori_loop(0, part // CHUNK, step, 0)

    def experts(l):
        again = 0 if l == 0 else 12
        steps = 8 if l == 0 else 16

        def slice_at(i):
            return i if l == 0 else jnp.where(i < again, lax.rem(i, 4), i - 8)

        def low(i):
            return jnp.int32(0) if l == 0 else jnp.where(i < again, i // 4, 0)

        def high(i):
            return jnp.int32(4) if l == 0 else jnp.where(i < 4, 1, jnp.where(i < 8, 2, 4))

        def first_use(i):
            return i >= 0 if l == 0 else jnp.logical_or(i < 4, i >= again)

        def prefetch(i):
            waits = (3, 5) if l == 0 else (13,)
            fine = i < steps - 1
            for k in waits:
                fine = jnp.logical_and(fine, i != k)
            return fine

        def ready(i, pieces):
            for s in range(1, 8):
                @pl.when(jnp.logical_and(first_use(i), slice_at(i) == s))
                def _(s=s):
                    for t in pieces:
                        if s % 2:
                            arrived(l, t, s)
                        elif (l, t, s // 2) not in early:
                            pass_ring(l, t, s // 2)

        early = {(0, 0, 1), (0, 1, 1), (0, 2, 1), (1, 0, 1), (1, 1, 1), (1, 2, 1), (1, 0, 2), (1, 1, 2), (1, 2, 2)}

        def at(i, k, action):
            @pl.when(i == k)
            def _():
                action()

        def step(i, carry):
            @pl.when(i < steps)
            def _():
                load13_wait()

            def gate_up(rb, c):
                @pl.when(jnp.logical_and(rb == jnp.where(i == steps - 1, high(i) - 1, low(i)), i > 0))
                def _():
                    ready(i - 1, (2,))
                    load2(l, slice_at(i - 1))

                @pl.when(jnp.logical_and(rb == high(i) - 1, prefetch(i)))
                def _():
                    ready(i + 1, (0, 1))
                    load13(l, slice_at(i + 1), i + 1)
                if l == 0:
                    @pl.when(jnp.logical_and(rb == 3, i == 0))
                    def _():
                        pass_ring(0, 2, 1)
                for c, width in groups[:-1]:
                    last = c + width == main
                    span = pl.ds(2 * c, 2 * width + (2 * tail if last else 0))
                    both = lax.dot_general(h_all[rb], b13[lax.rem(i, 2), span, :], NT,
                                           preferred_element_type=jnp.float32)
                    u, v = both[:, :width], both[:, width:2 * width]
                    act[lax.rem(i, 2), rb, :, c:c + width] = (u * jax.nn.sigmoid(u) * v).astype(jnp.bfloat16)
                    if last:
                        edge = both[:, 2 * width:]
                        rest = edge * jax.nn.sigmoid(edge) * pltpu.roll(edge, tail, 1)
                        act[lax.rem(i, 2), rb, :, main:] = rest[:, :tail].astype(jnp.bfloat16)
                return c
            lax.fori_loop(low(i), jnp.where(i < steps, high(i), low(i)), gate_up, 0)

            @pl.when(i == steps)
            def _():
                ready(i - 1, (2,))
                load2(l, slice_at(i - 1))

            if l == 0:
                @pl.when(i == 5)
                def _():
                    for t in range(3):
                        push_own(1, t)

            def fetch_next(late):
                @pl.when(jnp.logical_and(jnp.logical_and(i < steps - 1, jnp.logical_not(prefetch(i))), (i == 5) == late))
                def _():
                    ready(i + 1, (0, 1))
                    load13(l, slice_at(i + 1), i + 1)

            fetch_next(False)

            @pl.when(i > 0)
            def _():
                load2_wait()

            def down_proj(rb, c):
                cols = 512
                for n in range(d_model // cols):
                    span = pl.ds(n * cols, cols)
                    acc[rb, :, span] += jnp.dot(act[lax.rem(i + 1, 2), rb], b2[:, span],
                                                preferred_element_type=jnp.float32)

                @pl.when(jnp.logical_and(i == steps, rb == 1))
                def _():
                    issue_outputs(l, 0)
                return c
            lax.fori_loop(low(i - 1), jnp.where(i > 0, high(i - 1), low(i - 1)), down_proj, 0)

            fetch_next(True)
            return carry

        def second_half():
            combine(0, 1)
            for i in (0, 1):
                send_side(0, 1, i).wait_send()
            normalise(1, 1)
            send_hidden(1, 1)
            clear_acc(1)
            pass_ring(1, 0, 2)

        def far_rows():
            load_sides(1, 1)
            take_far(1, 1)

        def step_all(i, carry):
            if l == 1:
                at(i, 2, second_half)
                at(i, 4, lambda: take_far(1, 0))
                at(i, 5, lambda: pass_ring(1, 1, 2))
                at(i, 6, lambda: take_sides(1, 1))
                at(i, 8, far_rows)
                at(i, 9, lambda: pass_ring(1, 2, 2))
            return step(i, carry)

        load13(l, 0, jnp.int32(0))
        lax.fori_loop(0, steps + 1, step_all, 0)

    barrier = pltpu.get_barrier_semaphore()
    for dev in (to_next, to_prev, to_partner, to_up, to_down):
        pl.semaphore_signal(barrier, inc=1, device_id=dev, device_id_type=MESH)
    pl.semaphore_wait(barrier, 5)

    for t in range(3):
        push_own(0, t)
    x_copy = pltpu.make_async_copy(x_hbm, xs, ld.at[3])
    x_copy.start()
    x_copy.wait()
    for q in (0, 1):
        normalise(0, q)
        send_hidden(0, q)
    for q in (0, 1):
        take_sides(0, q)
        clear_acc(q)
    pass_ring(0, 0, 1)
    for q in (0, 1):
        load_sides(0, q)
        take_far(0, q)
    pass_ring(0, 1, 1)
    experts(0)

    relay(0, 0)
    issue_outputs(0, 1)
    combine(0, 0)
    for i in (0, 1):
        send_side(0, 0, i).wait_send()
    normalise(1, 0)
    send_hidden(1, 0)
    clear_acc(0)
    relay(0, 1)
    for t in range(3):
        pass_ring(1, t, 1)
    take_sides(1, 0)
    load_sides(1, 0)
    experts(1)

    relay(1, 0)
    issue_outputs(1, 1)
    combine(1, 0)
    outs = [pltpu.make_async_copy(xs.at[pl.ds(q * part, part)], out_hbm.at[pl.ds(q * part, part)], ld.at[2 + q])
            for q in (0, 1)]
    outs[0].start()
    relay(1, 1)
    combine(1, 1)
    outs[1].start()
    for l in range(layers):
        for t in range(3):
            for r in range(3):
                ring_send(l, t, r).wait_send()
            for r in range(4):
                partner_send(l, t, r).wait_send()
        for q in (0, 1):
            for i in (0, 1):
                if l == 1:
                    send_side(l, q, i).wait_send()
                send_far(l, q, i).wait_send()
            for i in range(4 if l == 1 else 0):
                output_copy(l, q, i).wait_send()
            for i in (4, 5):
                output_copy(l, q, i).wait_send()
    outs[0].wait()
    outs[1].wait()


def solution(mesh):
    n_ep, n_fs = mesh.shape["ep"], mesh.shape["fsdp"]
    token_spec = P(("rep", "ep", "fsdp"), None)
    expert_in_spec = P(None, "ep", None, "fsdp")
    expert_out_spec = P(None, "ep", "fsdp", None)
    route_spec = P(None, ("rep", "ep", "fsdp"), None)

    def device_step(x_in, norm_w, router_w, gate_w, up_w, down_w, routes):
        layers, tok_dev, top_k = routes.shape
        d_model = x_in.shape[1]
        ff = down_w.shape[2]
        bf16 = jnp.bfloat16
        hbm, vmem = pl.BlockSpec(memory_space=pl.ANY), pl.BlockSpec(memory_space=pltpu.VMEM)
        shape = jax.ShapeDtypeStruct
        outs = pl.pallas_call(
            functools.partial(kernel, n_ep, n_fs),
            name="moe_layers",
            out_shape=(shape((tok_dev, d_model), bf16),
                       shape((layers, n_fs, ff, d_model), bf16),
                       shape((layers, n_fs, ff, d_model), bf16),
                       shape((layers, n_fs, ff, d_model), bf16),
                       shape((layers, 2, 3, tok_dev // 2, d_model), bf16),
                       shape((layers, 2, 3, tok_dev // 2, d_model), bf16),
                       shape((layers, 2, 2, tok_dev // 4, d_model), bf16)),
            in_specs=[hbm, vmem, vmem, hbm, hbm, hbm, vmem],
            out_specs=(hbm,) * 7,
            scratch_shapes=[
                pltpu.VMEM((4, tok_dev, d_model), bf16),
                pltpu.VMEM((4, tok_dev, d_model), jnp.float32),
                pltpu.VMEM((2, 2 * ff, d_model), bf16),
                pltpu.VMEM((ff, d_model), bf16),
                pltpu.VMEM((2, 4, tok_dev, ff), bf16),
                pltpu.VMEM((tok_dev, d_model), bf16),
                pltpu.VMEM((3, tok_dev // 2, d_model), bf16),
                pltpu.VMEM((tok_dev, 128), jnp.float32),
                pltpu.SemaphoreType.DMA((layers, 3, 7)),
                pltpu.SemaphoreType.DMA((layers, 3, 8)),
                pltpu.SemaphoreType.DMA((layers, 2, 4)),
                pltpu.SemaphoreType.DMA((layers, 2, 4)),
                pltpu.SemaphoreType.DMA((layers, 2, 6)),
                pltpu.SemaphoreType.DMA((layers, 2, 6)),
                pltpu.SemaphoreType.DMA((10,)),
            ],
            compiler_params=pltpu.CompilerParams(collective_id=0, has_side_effects=True,
                                                 vmem_limit_bytes=66_000_000),
        )(x_in, norm_w, jnp.swapaxes(router_w, 1, 2), jnp.swapaxes(gate_w, 2, 3), jnp.swapaxes(up_w, 2, 3), down_w, routes)
        return outs[0]

    return jax.shard_map(device_step, mesh=mesh,
                         in_specs=(token_spec, P(), P(), expert_in_spec, expert_in_spec, expert_out_spec, route_spec),
                         out_specs=token_spec, check_vma=False)
```

time: 993 us -> 701 us (0.71)
  Pallas kernels: 0 us -> 696 us
  waiting for transfers between devices: 422 us -> 0 us
  matrix products: 367 us -> 0 us
  local copies, waits for them, and re-layouts: 119 us -> 4.87 us
  other arithmetic: 38.6 us -> 0 us
  starting transfers between devices: 23.9 us -> 0 us
  between operations: 14.5 us -> 0.01 us
    pallas_call x0 -> x1, Pallas kernels: none -> 696 us  [device_step(): pl.pallas_call(functools.partial(kernel, n_ep, n_fs), name='moe_layers',...]
    dot_general x8 -> x0, matrix products: 367 us -> none  [the longest x2 138 us: expert_ffn(): jnp.einsum('erd,edf->erf', expert_rows, up_full, preferred_element_type=j...]
    all_to_all x4 -> x0, waiting for transfers between devices: 346 us -> none  [the longest x2 188 us: device_step(): recv_buf = lax.all_to_all(send_buf, 'ep', 1, 1, tiled=True)]
    all_gather x6 -> x0, waiting for transfers between devices: 74.1 us -> none  [the longest x2 43 us: device_step(): down_full = lax.all_gather(down_w[layer_idx], 'fsdp', axis=1, tiled=True)]
    gather x10 -> x0, local copies, waits for them, and re-layouts: 67.5 us -> none  [the longest x2 26.7 us: device_step(): back_buf.reshape(experts * capacity, d_model)[pair_slot]]
    reduce_sum x8 -> x0, other arithmetic: 30 us -> none  [the longest x2 28.3 us: combine(): jnp.sum(gate_probs[..., None] * pair_out.astype(jnp.float32), axis=-2)]
    all_to_all x4 -> x0, starting transfers between devices: 23.7 us -> none  [the longest x2 12.1 us: device_step(): lax.all_to_all(expert_out.reshape(n_local, owners, capacity, d_model), 'e...]
    slice x6 -> x0, local copies, waits for them, and re-layouts: 20.1 us -> none  [the longest x1 6.29 us: device_step(): down_full = lax.all_gather(down_w[layer_idx], 'fsdp', axis=1, tiled=True)]
  transfers between devices with their start and end apart: 10 -> 0, of which waited for: 6 -> 0; matrix products, arithmetic and copies ran while one was open for 43% -> 0% of each run, Pallas kernels for 0% -> 0%
where the time goes in v2:
time: 701 us
  Pallas kernels  696 us (99%)
    pallas_call x1, Pallas kernels, device_step(): pl.pallas_call(functools.partial(kernel, n_ep, n_fs), name='moe_layers',...  696 us

profile of v2, /device:TPU:98, one launch (start us, length us, event | category | flops | bytes accessed | tf_op | source)
XLA Modules:
  0.0 700.6 jit_solution(14015446823572650945)
XLA Ops:
  0.0 1.7 copy.8.routes_ref
  1.7 695.8 %moe_layers.1 = (bf16[512,2048]{1,0:T(8,128)(2,1)}, bf16[2,8,704,2048]{3,2,1,0:T(8,128)(2,1)}, bf16[2,8,704,2048]{3,2,1,0:T(8,128)(2,1)}, bf16[2,8,704,2048]{3,2...) custom-call(bf16[512,2048]{1,0:T(8,128)(2,1)} %x_hbm.1, ...), custom_call_target="tpu_custom_call" | custom-call | tf_op jit(solution)/shard_map/moe_layers/pallas_call | solution.py:458
  697.5 3.2 copy.10
